TPU v7x, 256 devices: a whole 4x4x8 slice. The times are simulated.
256 devices in a mesh: band: 4 (over x_lo, core), fft: 64 (over y, z, x_hi).
Axes of the slice: x: 4 (x_hi: 2, x_lo: 2; x = x_hi * 2 + x_lo), y: 4, z: 8, core: 2. Of those that a mesh axis runs over, the one named last changes fastest.
Arguments:
- orbitals: bfloat16 [16, 2, 262144], P('band', None, 'fft'), may hold values from -6 to 6
- sphere_slot: int32 [262144], P('fft'), may hold values from 0 to 24575, as said below
- stick_column: int32 [8192], P('fft'), may hold values from 0 to 36863, as said below
- potential: float32 [192, 192, 192], P('fft'), may hold values from -3 to 3
- subspace: bfloat16 [64, 2, 262144], P('band', None, 'fft'), may hold values from -0.0234375 to 0.0234375
- previous: bfloat16 [16, 2, 262144], P('band', None, 'fft'), may hold values from -6 to 6
Outputs:
- applied: bfloat16 [16, 2, 262144], P('band', None, 'fft')
- intersection: float32 [2, 64, 16], P(None, 'fft', 'band')
Inputs may be any that keep to these rules, and one draw needn't show every extreme that they name: `sphere_slot`: within each aligned block of 4096 entries the values are distinct. `stick_column`: aligned block d of 128 entries holds distinct columns x * 192 + y with d * 3 <= x < (d + 1) * 3.
All inputs are finite; a program needn't handle non-finite values.
Results may differ from a plain program's by a relative error of at most 0.012.
Values may be sent and summed in bfloat16 or wider, within the bound.
A program may use at most 64 MiB of HBM per device.

v0:
```python
import functools
import math

import jax
import jax.numpy as jnp
import numpy as np
from jax import lax
from jax.experimental import pallas as pl
from jax.experimental.pallas import tpu as pltpu
from jax.sharding import PartitionSpec as P

F32 = jnp.float32
BF16 = jnp.bfloat16
NT = (((1,), (1,)), ((), ()))


def dot(a, b):
    return jnp.dot(a, b, preferred_element_type=F32)


def dot_nt(a, b):
    return lax.dot_general(a, b, NT, preferred_element_type=F32)


def tables(grid, owners):
    depth = grid // owners
    groups = owners // 4
    k = np.arange(grid)
    angle = 2.0 * math.pi * ((k[:, None] * k[None, :]) % grid) / grid
    cos, sin = np.cos(angle), np.sin(angle)
    icos, isin = cos / grid, -sin / grid
    zorder = np.arange(grid)
    zorder = (zorder % owners) * depth + zorder // owners
    rows = np.full(groups * 16, -1)
    for g in range(groups):
        rows[16 * g : 16 * g + 4 * depth] = 4 * depth * g + np.arange(4 * depth)

    def padded(table):
        out = np.zeros((groups * 16, grid))
        out[rows >= 0] = table[rows[rows >= 0]]
        return out

    def trio(c, s):
        return [jnp.asarray(t, BF16) for t in (c, s, -s)]

    zf = trio(cos[zorder], sin[zorder])
    zb = trio(icos[zorder], isin[zorder])
    yf = trio(cos, sin)
    yb = trio(icos, isin)
    xf = trio(padded(cos).T, padded(sin).T)
    xb = trio(padded(icos), padded(isin))
    return zf, zb, yf, yb, xf, xb


def vmem():
    return pl.BlockSpec(memory_space=pltpu.VMEM)


def call(body, outs, scratch, name):
    single = not isinstance(outs, (list, tuple))
    return pl.pallas_call(
        body,
        out_shape=outs,
        out_specs=vmem() if single else [vmem() for _ in outs],
        scratch_shapes=scratch,
        compiler_params=pltpu.CompilerParams(vmem_limit_bytes=60 * 2**20),
        name=name,
    )


def forward_z(orb, slot, zf, send, stick_hot, plane_hot, stage):
    bands = orb.shape[0] // 2
    sticks, grid = stick_hot.shape[0], plane_hot.shape[0]
    owners = send.shape[0]
    depth = grid // owners
    rows = 2 * bands * depth
    chunk = 512
    for c in range(0, slot.shape[1], chunk):
        sl = slot[:, c : c + chunk]
        stick = lax.rem(sl, sticks)
        plane = lax.div(sl, sticks)
        stick_hot[:, c : c + chunk] = (
            lax.broadcasted_iota(jnp.int32, (sticks, chunk), 0) == stick
        ).astype(F32).astype(BF16)
        plane_hot[:, c : c + chunk] = (
            lax.broadcasted_iota(jnp.int32, (grid, chunk), 0) == plane
        ).astype(F32).astype(BF16)
    zc, zs, zn = (t[...] for t in zf)
    for b in range(bands):
        parts = []
        for p in range(2):
            lhs = stick_hot[...] * orb[2 * b + p : 2 * b + p + 1, :]
            parts.append(dot_nt(lhs, plane_hot[...]).astype(BF16))
        re, im = parts
        out = (
            dot_nt(zc, re) + dot_nt(zn, im),
            dot_nt(zs, re) + dot_nt(zc, im),
        )
        for p in range(2):
            for z in range(depth):
                row = (p * bands + b) * depth + z
                stage[pl.ds(row, owners, stride=rows), :] = out[p][z * owners : (z + 1) * owners]
    for f in range(owners):
        send[f] = stage[rows * f : rows * (f + 1), :].astype(BF16)


def build_masks(cols, ymask, xmask, grid, depth):
    groups = ymask.shape[0]
    sticks = cols.shape[1]
    for g in range(groups):
        for d in range(4):
            col = cols[4 * g + d : 4 * g + d + 1, :]
            x = lax.div(col, grid)
            y = col - x * grid
            x = x - 4 * depth * g
            lanes = slice(sticks * d, sticks * (d + 1))
            ymask[g, :, lanes] = (
                lax.broadcasted_iota(jnp.int32, (grid, sticks), 0) == y
            ).astype(F32).astype(BF16)
            xmask[g, :, lanes] = (
                lax.broadcasted_iota(jnp.int32, (16, sticks), 0) == x
            ).astype(F32)


def plane_work(recv, pot, yf, yb, xf, xb, send, ymask, xmask, val, are, aim, back):
    groups = ymask.shape[0]
    rows = recv.shape[1]
    half = rows // 2
    depth = pot.shape[0]
    sticks = recv.shape[2]
    grid = pot.shape[1]
    wide = 4 * sticks

    def scatter(g, carry):
        for d in range(4):
            val[:, sticks * d : sticks * (d + 1)] = recv[4 * g + d].astype(F32)
        mask = xmask[g]
        parts = []
        for p in range(2):
            lhs = jnp.concatenate(
                [(mask * val[r : r + 1, :]).astype(BF16) for r in range(p * half, (p + 1) * half)],
                axis=0,
            )
            parts.append(dot_nt(lhs, ymask[g]).astype(BF16))
        re, im = parts
        at = pl.ds(pl.multiple_of(16 * g, 16), 16)
        are[:, at, :] = (dot(re, yf[0][...]) + dot(im, yf[2][...])).astype(BF16).reshape(half, 16, grid)
        aim[:, at, :] = (dot(re, yf[1][...]) + dot(im, yf[0][...])).astype(BF16).reshape(half, 16, grid)
        return carry

    lax.fori_loop(0, groups, scatter, 0)

    def local(r, carry):
        z = lax.rem(r, depth)
        v = pot[z]
        re, im = are[r], aim[r]
        wr = ((dot(xf[0][...], re) + dot(xf[2][...], im)) * v).astype(BF16)
        wi = ((dot(xf[1][...], re) + dot(xf[0][...], im)) * v).astype(BF16)
        br = (dot(xb[0][...], wr) + dot(xb[2][...], wi)).astype(BF16)
        bi = (dot(xb[1][...], wr) + dot(xb[0][...], wi)).astype(BF16)
        back[r] = (dot(br, yb[0][...]) + dot(bi, yb[2][...])).astype(BF16)
        back[half + r] = (dot(br, yb[1][...]) + dot(bi, yb[0][...])).astype(BF16)
        return carry

    lax.fori_loop(0, half, local, 0)

    def pick(g, carry):
        mask = xmask[g]
        at = pl.ds(pl.multiple_of(16 * g, 16), 16)
        lhs = back[:, at, :].reshape(rows * 16, grid)
        t = dot(lhs, ymask[g]).reshape(rows, 16, wide)
        got = jnp.sum(t * mask[None], axis=1)
        for d in range(4):
            send[4 * g + d] = got[:, sticks * d : sticks * (d + 1)].astype(BF16)
        return carry

    lax.fori_loop(0, groups, pick, 0)


def frequency(values, grid):
    return jnp.where(values >= grid // 2, values - grid, values).astype(F32)


def backward_z(recv, orb, slot, column, zb, out, stage, stick_hot, plane_hot):
    owners, rows, sticks = recv.shape
    bands = orb.shape[0] // 2
    grid = zb[0].shape[0]
    depth = grid // owners
    chunk = 512
    for f in range(owners):
        stage[rows * f : rows * (f + 1), :] = recv[f].astype(F32)
    col = column[...]
    x = lax.div(col, grid)
    y = col - x * grid
    coords = jnp.concatenate([x, y, x, y, x, y, x, y], axis=0).astype(F32).astype(BF16)
    lines = []
    zc, zs, zn = (t[...] for t in zb)
    for b in range(bands):
        parts = []
        for p in range(2):
            cut = []
            for z in range(depth):
                row = (p * bands + b) * depth + z
                cut.append(stage[pl.ds(row, owners, stride=rows), :])
            parts.append(jnp.concatenate(cut, axis=0).T.astype(BF16))
        re, im = parts
        lines.append((dot(re, zc) + dot(im, zn)).astype(BF16))
        lines.append((dot(re, zs) + dot(im, zc)).astype(BF16))
    for c in range(0, slot.shape[1], chunk):
        cut = slice(c, c + chunk)
        sl = slot[:, cut]
        stick = lax.rem(sl, sticks)
        plane = lax.div(sl, sticks)
        hot = lax.broadcasted_iota(jnp.int32, (sticks, chunk), 0) == stick
        phot = (lax.broadcasted_iota(jnp.int32, (grid, chunk), 0) == plane).astype(F32).astype(BF16)
        shot = hot.astype(F32)
        xy = dot(coords, shot.astype(BF16))
        fz = frequency(plane, grid)
        fx = frequency(xy[0:1].astype(jnp.int32), grid)
        fy = frequency(xy[1:2].astype(jnp.int32), grid)
        kinetic = (fz * fz + fx * fx + fy * fy) * (2.0 / (grid * grid))
        got = []
        for line in lines:
            t = dot(line, phot)
            got.append(jnp.sum(t * shot, axis=0, keepdims=True))
        out[:, cut] = (
            jnp.concatenate(got, axis=0) + kinetic * orb[:, cut].astype(F32)
        ).astype(BF16)


def kernel_one(orb, slot, zc, zs, zn, send, stick_hot, plane_hot, stage):
    forward_z(orb, slot, (zc, zs, zn), send, stick_hot, plane_hot, stage)


def kernel_two(recv, cols, pot, *rest):
    yf, yb, xf, xb = (rest[3 * i : 3 * i + 3] for i in range(4))
    send, ymask, xmask, val, are, aim, back = rest[12:]
    build_masks(cols, ymask, xmask, pot.shape[1], pot.shape[0])
    plane_work(recv, pot, yf, yb, xf, xb, send, ymask, xmask, val, are, aim, back)


def kernel_three(recv, orb, slot, column, zc, zs, zn, out, stage):
    backward_z(recv, orb, slot, column, (zc, zs, zn), out, stage, None, None)


def per_device(orbitals, sphere_slot, stick_column, potential, subspace, previous):
    owners = lax.axis_size("fft")
    groups = owners // 4
    grid = potential.shape[1]
    depth = potential.shape[0]
    sticks = stick_column.shape[0]
    waves = sphere_slot.shape[0]
    bands = orbitals.shape[0]
    rows = 2 * bands * depth
    zf, zb, yf, yb, xf, xb = tables(grid, owners)
    orb = orbitals.reshape(2 * bands, waves)
    slot = sphere_slot.reshape(1, waves)
    column = stick_column.reshape(1, sticks)

    def sds(shape, kind):
        return jax.ShapeDtypeStruct(shape, kind)

    message = sds((owners, rows, sticks), BF16)
    send = call(
        kernel_one,
        message,
        [
            pltpu.VMEM((sticks, waves), BF16),
            pltpu.VMEM((grid, waves), BF16),
            pltpu.VMEM((owners * rows, sticks), F32),
        ],
        "forward_z",
    )(orb, slot, *zf)
    cols = lax.all_gather(stick_column, "fft")
    recv = lax.all_to_all(send, "fft", 0, 0, tiled=True)
    send = call(
        kernel_two,
        message,
        [
            pltpu.VMEM((groups, grid, 4 * sticks), BF16),
            pltpu.VMEM((groups, 16, 4 * sticks), F32),
            pltpu.VMEM((rows, 4 * sticks), F32),
            pltpu.VMEM((rows // 2, groups * 16, grid), BF16),
            pltpu.VMEM((rows // 2, groups * 16, grid), BF16),
            pltpu.VMEM((rows, groups * 16, grid), BF16),
        ],
        "planes",
    )(recv, cols, potential, *yf, *yb, *xf, *xb)
    recv = lax.all_to_all(send, "fft", 0, 0, tiled=True)
    applied = call(
        kernel_three,
        sds((2 * bands, waves), BF16),
        [pltpu.VMEM((owners * rows, sticks), F32)],
        "backward_z",
    )(recv, orb, slot, column, *zb)
    applied = applied.reshape(orbitals.shape)

    every = lax.all_gather(previous, "band")
    every = every.reshape(-1, 2, waves)
    sr, si = subspace[:, 0], subspace[:, 1]
    pr, pi = every[:, 0], every[:, 1]
    own = jnp.stack([dot_nt(sr, pr) + dot_nt(si, pi), dot_nt(sr, pi) - dot_nt(si, pr)])
    groups_of = lax.axis_size("band")
    tiles = own.reshape(2, own.shape[1], groups_of, bands)
    tiles = lax.all_to_all(jnp.moveaxis(tiles, 2, 0), "band", 0, 0, tiled=True)
    tiles = jnp.moveaxis(tiles, 1, 2).reshape(-1, 2, bands)
    tiles = lax.all_to_all(tiles[:, None], "fft", 0, 1, tiled=True)
    intersection = jnp.moveaxis(jnp.sum(tiles, axis=1), 0, 1)
    return applied, intersection


def solution(mesh):
    return jax.shard_map(
        per_device,
        mesh=mesh,
        in_specs=(
            P("band", None, "fft"),
            P("fft"),
            P("fft"),
            P("fft", None, None),
            P("band", None, "fft"),
            P("band", None, "fft"),
        ),
        out_specs=(P("band", None, "fft"), P(None, "fft", "band")),
        check_vma=False,
    )
```

profile of v0, /device:TPU:8, one launch (start us, length us, event | category | flops | bytes accessed | tf_op | source)
XLA Modules:
  0.0 296.4 jit_solution(13342745643594263691)
XLA Ops:
  0.6 6.0 %all-gather.1 = bf16[16,2,4096]{2,1,0:T(2,128)(2,1)S(1)} all-gather(bf16[4,2,4096]{2,1,0:T(2,128)(2,1)} %param.29), channel_id=3, replica_groups=mesh['band'=4,'fft'=64] {'band'}, dimensions={0}, use_global_device_ids=true | all-gather | bytes 327680 | tf_op jit(solution)/shard_map/all_gather | solution.py:298
  6.6 0.0 copy-start.2
  6.6 0.6 fusion.3
  7.2 0.4 copy-done.2
  7.6 0.5 fusion.2
  8.1 0.4 fusion.1
  8.5 0.4 fusion
  8.9 0.4 convolution_add_fusion
  9.3 0.1 copy.40
  9.4 0.4 convolution_subtract_fusion
  9.8 0.0 copy-start.3
  9.8 0.1 copy.41
  9.9 0.7 reshape.36
  10.5 3.2 %all-to-all-start.2 = ((f32[4,1,128]{2,1,0:T(1,128)}), f32[4,1,128]{2,1,0:T(1,128)S(1)}, u32[]{:S(2)}, u32[]{:S(2)}) async-start(f32[4,1,128]{2,1,0:T(1,128)} %reshape.36), calls=%async_computation.2 | async-start | bytes 4096 | tf_op jit(solution)/shard_map/all_to_all | solution.py:305
  13.8 0.0 copy-done.3
  13.8 0.7 reshape.26.orb
  14.4 7.0 %forward_z.1 = bf16[64,24,128]{2,1,0:T(8,128)(2,1)} custom-call(bf16[8,4096]{1,0:T(8,128)(2,1)} %reshape.26.orb, s32[1,4096]{1,0:T(1,128)} %bitcast.36, bf16[192,192]{1,0:T(8,128)(2,1)} %constant.38.clone.zc, bf16[192,192]{1,0:T(8,128)(2,1)} %constant.39.clone.zs, bf16[192,192]{1,0:T(8,128)(2,1)} %constant.40.clone.zn), custom_call_target="tpu_custom_call" | custom-call | tf_op jit(solution)/shard_map/forward_z/pallas_call | solution.py:264
  21.5 0.0 all-to-all-done.2
  21.5 14.5 %all-to-all-start = ((bf16[64,24,128]{2,1,0:T(8,128)(2,1)}), bf16[64,24,128]{2,1,0:T(8,128)(2,1)S(1)}, u32[]{:S(2)}, u32[]{:S(2)}) async-start(bf16[64,24,128]{2,1,0:T(8,128)(2,1)} %forward_z.1), calls=%async_computation | async-start | bytes 786432 | tf_op jit(solution)/shard_map/all_to_all | solution.py:275
  36.0 0.5 broadcast
  36.5 0.7 reduce.3
  37.2 0.1 reshape.37
  37.3 0.8 copy.46
  38.1 14.1 %all-to-all-done.recv = bf16[64,24,128]{2,1,0:T(8,128)(2,1)S(1)} async-done(((bf16[64,24,128]{2,1,0:T(8,128)(2,1)}), bf16[64,24,128]{2,1,0:T(8,128)(2,1)S(1)}, u32[]{:S(2)}, u32[]{:S(2)}) %all-to-all-start) | async-done | bytes 393248 | tf_op jit(solution)/shard_map/all_to_all | solution.py:275
  52.2 0.0 copy-start.1
  52.2 6.8 %all-to-all-start.3 = ((f32[64,1,2,4]{3,2,1,0:T(2,128)}), f32[64,1,2,4]{3,2,1,0:T(2,128)S(1)}, u32[]{:S(2)}, u32[]{:S(2)}) async-start(f32[64,1,2,4]{3,2,1,0:T(2,128)} %bitcast.12), calls=%async_computation.3 | async-start | bytes 131072 | tf_op jit(solution)/shard_map/all_to_all | solution.py:307
  59.1 0.0 copy-start.4
  59.1 0.6 copy-done.4
  59.7 164.9 %all-gather.2 = s32[64,1,128]{2,1,0:T(1,128)} all-gather(s32[1,1,128]{2,1,0:T(1,128)S(1)} %bitcast.41), channel_id=2, replica_groups=mesh['band'=4,'fft'=64] {'fft'}, dimensions={0}, use_global_device_ids=true | all-gather | bytes 33280 | tf_op jit(solution)/shard_map/all_gather | solution.py:274
  224.6 0.0 copy-done.1
  224.6 24.9 %planes.1 = bf16[64,24,128]{2,1,0:T(8,128)(2,1)} custom-call(bf16[64,24,128]{2,1,0:T(8,128)(2,1)} %copy-done.1, s32[64,128]{1,0:T(8,128)} %bitcast.35, f32[3,192,192]{2,1,0:T(8,128)} %pot.1, bf16[192,192]{1,0:T(8,128)(2,1)} %constant.44.clone.rest_0_, bf16[192,192]{1,0:T(8,128)(2,1)} %constant.45.clone.rest_1_, bf16[192,192]{1,0:T(8,128)(2,1)} %constant.46.clone.rest_2_, ...), custom_call_target="tpu_custom_call" | custom-call | tf_op jit(solution)/shard_map/planes/pallas_call | solution.py:276
  249.5 0.0 all-to-all-done.3
  249.5 26.4 %all-to-all-start.1 = ((bf16[64,24,128]{2,1,0:T(8,128)(2,1)}), bf16[64,24,128]{2,1,0:T(8,128)(2,1)S(1)}, u32[]{:S(2)}, u32[]{:S(2)}) async-start(bf16[64,24,128]{2,1,0:T(8,128)(2,1)} %planes.1), calls=%async_computation.1 | async-start | bytes 786432 | tf_op jit(solution)/shard_map/all_to_all | solution.py:289
  275.8 0.6 reduce_sum.9
  276.5 12.2 %all-to-all-done.1.recv = bf16[64,24,128]{2,1,0:T(8,128)(2,1)S(1)} async-done(((bf16[64,24,128]{2,1,0:T(8,128)(2,1)}), bf16[64,24,128]{2,1,0:T(8,128)(2,1)S(1)}, u32[]{:S(2)}, u32[]{:S(2)}) %all-to-all-start.1) | async-done | bytes 393248 | tf_op jit(solution)/shard_map/all_to_all | solution.py:289
  288.7 0.0 copy-start
  288.7 0.7 copy-done
  289.4 5.5 %backward_z.1 = bf16[8,4096]{1,0:T(8,128)(2,1)} custom-call(bf16[64,24,128]{2,1,0:T(8,128)(2,1)} %copy-done, bf16[8,4096]{1,0:T(8,128)(2,1)} %reshape.26.orb, s32[1,4096]{1,0:T(1,128)} %bitcast.37, s32[1,128]{1,0:T(1,128)} %bitcast.40, bf16[192,192]{1,0:T(8,128)(2,1)} %constant.41.clone.zc, bf16[192,192]{1,0:T(8,128)(2,1)} %constant.42.clone.zs, ...), custom_call_target="tpu_custom_call" | custom-call | tf_op jit(solution)/shard_map/backward_z/pallas_call | solution.py:290
  294.9 1.5 reshape.28
  (2 shorter events, 0.0 us)
Async XLA Ops:
  6.6 1.0 copy-start.2
  9.8 4.0 %copy-start.3 = (bf16[4,2,4096]{2,1,0:T(2,128)(2,1)S(1)}, bf16[4,2,4096]{2,1,0:T(2,128)(2,1)}, u32[]{:S(2)}) copy-start(bf16[4,2,4096]{2,1,0:T(2,128)(2,1)} %param.24) | copy-start | bytes 196612
  10.5 10.9 %all-to-all-start.2 = ((f32[4,1,128]{2,1,0:T(1,128)}), f32[4,1,128]{2,1,0:T(1,128)S(1)}, u32[]{:S(2)}, u32[]{:S(2)}) async-start(f32[4,1,128]{2,1,0:T(1,128)} %reshape.36), calls=%async_computation.2 | async-start | bytes 4096 | tf_op jit(solution)/shard_map/all_to_all | solution.py:305
  21.5 30.7 %all-to-all-start = ((bf16[64,24,128]{2,1,0:T(8,128)(2,1)}), bf16[64,24,128]{2,1,0:T(8,128)(2,1)S(1)}, u32[]{:S(2)}, u32[]{:S(2)}) async-start(bf16[64,24,128]{2,1,0:T(8,128)(2,1)} %forward_z.1), calls=%async_computation | async-start | bytes 786432 | tf_op jit(solution)/shard_map/all_to_all | solution.py:275
  52.2 172.4 %copy-start.1 = (bf16[64,24,128]{2,1,0:T(8,128)(2,1)}, bf16[64,24,128]{2,1,0:T(8,128)(2,1)S(1)}, u32[]{:S(2)}) copy-start(bf16[64,24,128]{2,1,0:T(8,128)(2,1)S(1)} %all-to-all-done.recv) | copy-start | bytes 1179652
  52.2 197.3 %all-to-all-start.3 = ((f32[64,1,2,4]{3,2,1,0:T(2,128)}), f32[64,1,2,4]{3,2,1,0:T(2,128)S(1)}, u32[]{:S(2)}, u32[]{:S(2)}) async-start(f32[64,1,2,4]{3,2,1,0:T(2,128)} %bitcast.12), calls=%async_computation.3 | async-start | bytes 131072 | tf_op jit(solution)/shard_map/all_to_all | solution.py:307
  59.1 0.7 copy-start.4
  249.5 39.2 %all-to-all-start.1 = ((bf16[64,24,128]{2,1,0:T(8,128)(2,1)}), bf16[64,24,128]{2,1,0:T(8,128)(2,1)S(1)}, u32[]{:S(2)}, u32[]{:S(2)}) async-start(bf16[64,24,128]{2,1,0:T(8,128)(2,1)} %planes.1), calls=%async_computation.1 | async-start | bytes 786432 | tf_op jit(solution)/shard_map/all_to_all | solution.py:289
  288.7 0.7 copy-start
where the time goes:
time: 297 us; the launch traced here: 296 us
  blocking collectives  171 us (58%)
  starting transfers between devices  51 us (17%)
  Pallas kernels  37.4 us (13%)
  waiting for transfers between devices  26.3 us (9%)
  local copies, waits for them, and re-layouts  7.26 us (2%)
    all_gather x1, blocking collectives, per_device(): cols = lax.all_gather(stick_column, 'fft')  165 us
    all_to_all x2, starting transfers between devices, per_device(): recv = lax.all_to_all(send, 'fft', 0, 0, tiled=True)  40.9 us
    all_to_all x2, waiting for transfers between devices, per_device(): recv = lax.all_to_all(send, 'fft', 0, 0, tiled=True)  26.3 us
    pallas_call x1, Pallas kernels, per_device(): call(kernel_two, message, [pltpu.VMEM((groups, grid, 4 * sticks), BF16),...  24.9 us
    pallas_call x1, Pallas kernels, per_device(): call(kernel_one, message, [pltpu.VMEM((sticks, waves), BF16), pltpu.VMEM(...  7.03 us
    all_to_all x1, starting transfers between devices, per_device(): tiles = lax.all_to_all(tiles[:, None], 'fft', 0, 1, tiled=True)  6.82 us
    all_gather x1, blocking collectives, per_device(): every = lax.all_gather(previous, 'band')  5.99 us
  transfers between devices with their start and end apart: 4, of which 2 were waited for; matrix products, arithmetic and copies ran while one was open for 1% of the time, Pallas kernels for 11%

commit v1 on v0

--- a/solution.py
+++ b/solution.py
@@ -271,7 +271,8 @@
         ],
         "forward_z",
     )(orb, slot, *zf)
-    cols = lax.all_gather(stick_column, "fft")
+    cols = jnp.broadcast_to(stick_column[None], (owners, sticks))
+    cols = lax.all_to_all(cols, "fft", 0, 0, tiled=True)
     recv = lax.all_to_all(send, "fft", 0, 0, tiled=True)
     send = call(
         kernel_two,

time: 297 us -> 134 us (0.45)
  blocking collectives: 171 us -> 12.3 us
  starting transfers between devices: 51 us -> 43.3 us
  waiting for transfers between devices: 26.3 us -> 30 us
    all_gather x1 -> x0, blocking collectives: 165 us -> none  [per_device(): cols = lax.all_gather(stick_column, 'fft')]
    all_to_all x2, starting transfers between devices: 40.9 us -> 22.2 us  [per_device(): recv = lax.all_to_all(send, 'fft', 0, 0, tiled=True)]
    all_to_all x1, starting transfers between devices: 3.24 us -> 14.3 us  [per_device(): cols = lax.all_to_all(cols, 'fft', 0, 0, tiled=True)]
    all_to_all x0 -> x1, blocking collectives: none -> 6.33 us  [per_device(): tiles = lax.all_to_all(jnp.moveaxis(tiles, 2, 0), 'band', 0, 0, tiled=True)]
    all_to_all x1, waiting for transfers between devices: 0.01 us -> 3.32 us  [per_device(): cols = lax.all_to_all(cols, 'fft', 0, 0, tiled=True)]
  transfers between devices with their start and end apart: 4 -> 4, of which waited for: 2 -> 3; matrix products, arithmetic and copies ran while one was open for 1% -> 2% of each run, Pallas kernels for 11% -> 24%
where the time goes in v1:
time: 134 us
  starting transfers between devices  43.3 us (32%)
  Pallas kernels  37.4 us (28%)
  waiting for transfers between devices  30 us (22%)
  blocking collectives  12.3 us (9%)
  local copies, waits for them, and re-layouts  7.28 us (5%)
  matrix products  1.57 us (1%)
    all_to_all x2, waiting for transfers between devices, per_device(): recv = lax.all_to_all(send, 'fft', 0, 0, tiled=True)  26.7 us
    pallas_call x1, Pallas kernels, per_device(): call(kernel_two, message, [pltpu.VMEM((groups, grid, 4 * sticks), BF16),...  24.9 us
    all_to_all x2, starting transfers between devices, per_device(): recv = lax.all_to_all(send, 'fft', 0, 0, tiled=True)  22.2 us
    all_to_all x1, starting transfers between devices, per_device(): cols = lax.all_to_all(cols, 'fft', 0, 0, tiled=True)  14.3 us
    pallas_call x1, Pallas kernels, per_device(): call(kernel_one, message, [pltpu.VMEM((sticks, waves), BF16), pltpu.VMEM(...  7.01 us
    all_to_all x1, starting transfers between devices, per_device(): tiles = lax.all_to_all(tiles[:, None], 'fft', 0, 1, tiled=True)  6.75 us
    all_to_all x1, blocking collectives, per_device(): tiles = lax.all_to_all(jnp.moveaxis(tiles, 2, 0), 'band', 0, 0, tiled=True)  6.33 us
    all_gather x1, blocking collectives, per_device(): every = lax.all_gather(previous, 'band')  5.99 us
  transfers between devices with their start and end apart: 4, of which 3 were waited for; matrix products, arithmetic and copies ran while one was open for 2% of the time, Pallas kernels for 24%

profile of v1, /device:TPU:8, one launch (start us, length us, event | category | flops | bytes accessed | tf_op | source)
XLA Modules:
  0.0 133.9 jit_solution(13020489627676057224)
XLA Ops:
  0.6 6.0 %all-gather = bf16[16,2,4096]{2,1,0:T(2,128)(2,1)S(1)} all-gather(bf16[4,2,4096]{2,1,0:T(2,128)(2,1)} %param.29), channel_id=2, replica_groups=mesh['band'=4,'fft'=64] {'band'}, dimensions={0}, use_global_device_ids=true | all-gather | bytes 327680 | tf_op jit(solution)/shard_map/all_gather | solution.py:299
  6.6 0.0 copy-start.2
  6.6 0.6 fusion.3
  7.2 0.4 copy-done.2
  7.6 0.5 fusion.2
  8.1 0.4 fusion.1
  8.5 0.4 fusion
  8.9 0.4 convolution_add_fusion
  9.3 0.1 copy.38
  9.4 0.4 convolution_subtract_fusion
  9.8 0.1 copy.39
  9.8 0.0 copy-start.5
  9.9 0.0 copy-start.4
  9.9 0.1 reshape.38
  10.0 6.3 %all_to_all.32 = f32[4,1,128]{2,1,0:T(1,128)S(1)} all-to-all(f32[4,1,128]{2,1,0:T(1,128)S(1)} %reshape.38), channel_id=1, replica_groups=mesh['band'=4,'fft'=64] {'band'}, dimensions={0} | all-to-all | bytes 4096 | tf_op jit(solution)/shard_map/all_to_all | solution.py:306
  16.3 0.0 copy-done.5
  16.3 0.6 broadcast_in_dim.8
  16.9 14.3 %all-to-all-start.1 = ((s32[64,1,128]{2,1,0:T(1,128)}), s32[64,1,128]{2,1,0:T(1,128)S(1)}, u32[]{:S(2)}, u32[]{:S(2)}) async-start(s32[64,1,128]{2,1,0:T(1,128)} %broadcast_in_dim.8), calls=%async_computation.1 | async-start | bytes 65536 | tf_op jit(solution)/shard_map/all_to_all | solution.py:275
  31.3 0.0 copy-done.4
  31.3 0.7 reshape.32.orb
  32.0 7.0 %forward_z.1 = bf16[64,24,128]{2,1,0:T(8,128)(2,1)} custom-call(bf16[8,4096]{1,0:T(8,128)(2,1)} %reshape.32.orb, s32[1,4096]{1,0:T(1,128)} %bitcast.35, bf16[192,192]{1,0:T(8,128)(2,1)} %constant.38.clone.zc, bf16[192,192]{1,0:T(8,128)(2,1)} %constant.39.clone.zs, bf16[192,192]{1,0:T(8,128)(2,1)} %constant.40.clone.zn), custom_call_target="tpu_custom_call" | custom-call | tf_op jit(solution)/shard_map/forward_z/pallas_call | solution.py:264
  39.0 3.3 %all-to-all-done.1 = s32[64,1,128]{2,1,0:T(1,128)S(1)} async-done(((s32[64,1,128]{2,1,0:T(1,128)}), s32[64,1,128]{2,1,0:T(1,128)S(1)}, u32[]{:S(2)}, u32[]{:S(2)}) %all-to-all-start.1) | async-done | bytes 32800 | tf_op jit(solution)/shard_map/all_to_all | solution.py:275
  42.3 0.0 copy-start.3
  42.3 0.6 copy-done.3
  42.9 9.4 %all-to-all-start = ((bf16[64,24,128]{2,1,0:T(8,128)(2,1)}), bf16[64,24,128]{2,1,0:T(8,128)(2,1)S(1)}, u32[]{:S(2)}, u32[]{:S(2)}) async-start(bf16[64,24,128]{2,1,0:T(8,128)(2,1)} %forward_z.1), calls=%async_computation | async-start | bytes 786432 | tf_op jit(solution)/shard_map/all_to_all | solution.py:276
  52.3 0.5 broadcast.3
  52.8 0.7 reduce.3
  53.5 0.1 reshape.39
  53.6 0.8 copy.44
  54.4 13.0 %all-to-all-done.recv = bf16[64,24,128]{2,1,0:T(8,128)(2,1)S(1)} async-done(((bf16[64,24,128]{2,1,0:T(8,128)(2,1)}), bf16[64,24,128]{2,1,0:T(8,128)(2,1)S(1)}, u32[]{:S(2)}, u32[]{:S(2)}) %all-to-all-start) | async-done | bytes 393248 | tf_op jit(solution)/shard_map/all_to_all | solution.py:276
  67.4 0.0 copy-start.1
  67.4 6.8 %all-to-all-start.4 = ((f32[64,1,2,4]{3,2,1,0:T(2,128)}), f32[64,1,2,4]{3,2,1,0:T(2,128)S(1)}, u32[]{:S(2)}, u32[]{:S(2)}) async-start(f32[64,1,2,4]{3,2,1,0:T(2,128)} %bitcast.11), calls=%async_computation.4 | async-start | bytes 131072 | tf_op jit(solution)/shard_map/all_to_all | solution.py:308
  74.1 0.0 copy-done.1
  74.1 24.9 %planes.1 = bf16[64,24,128]{2,1,0:T(8,128)(2,1)} custom-call(bf16[64,24,128]{2,1,0:T(8,128)(2,1)} %copy-done.1, s32[64,128]{1,0:T(8,128)} %bitcast.34, f32[3,192,192]{2,1,0:T(8,128)} %pot.1, bf16[192,192]{1,0:T(8,128)(2,1)} %constant.44.clone.rest_0_, bf16[192,192]{1,0:T(8,128)(2,1)} %constant.45.clone.rest_1_, bf16[192,192]{1,0:T(8,128)(2,1)} %constant.46.clone.rest_2_, ...), custom_call_target="tpu_custom_call" | custom-call | tf_op jit(solution)/shard_map/planes/pallas_call | solution.py:277
  99.0 0.0 all-to-all-done.4
  99.0 12.7 %all-to-all-start.2 = ((bf16[64,24,128]{2,1,0:T(8,128)(2,1)}), bf16[64,24,128]{2,1,0:T(8,128)(2,1)S(1)}, u32[]{:S(2)}, u32[]{:S(2)}) async-start(bf16[64,24,128]{2,1,0:T(8,128)(2,1)} %planes.1), calls=%async_computation.2 | async-start | bytes 786432 | tf_op jit(solution)/shard_map/all_to_all | solution.py:290
  111.8 0.6 reduce_sum.9
  112.4 13.7 %all-to-all-done.2.recv = bf16[64,24,128]{2,1,0:T(8,128)(2,1)S(1)} async-done(((bf16[64,24,128]{2,1,0:T(8,128)(2,1)}), bf16[64,24,128]{2,1,0:T(8,128)(2,1)S(1)}, u32[]{:S(2)}, u32[]{:S(2)}) %all-to-all-start.2) | async-done | bytes 393248 | tf_op jit(solution)/shard_map/all_to_all | solution.py:290
  126.1 0.0 copy-start
  126.1 0.7 copy-done
  126.9 5.5 %backward_z.1 = bf16[8,4096]{1,0:T(8,128)(2,1)} custom-call(bf16[64,24,128]{2,1,0:T(8,128)(2,1)} %copy-done, bf16[8,4096]{1,0:T(8,128)(2,1)} %reshape.32.orb, s32[1,4096]{1,0:T(1,128)} %bitcast.36, s32[1,128]{1,0:T(1,128)} %bitcast.39, bf16[192,192]{1,0:T(8,128)(2,1)} %constant.41.clone.zc, bf16[192,192]{1,0:T(8,128)(2,1)} %constant.42.clone.zs, ...), custom_call_target="tpu_custom_call" | custom-call | tf_op jit(solution)/shard_map/backward_z/pallas_call | solution.py:291
  132.3 1.5 %reshape.34 = bf16[4,2,4096]{2,1,0:T(2,128)(2,1)} reshape(bf16[8,4096]{1,0:T(8,128)(2,1)} %backward_z.1) | data formatting | bytes 131072 | tf_op jit(solution)/shard_map/reshape | solution.py:297
  (2 shorter events, 0.0 us)
Async XLA Ops:
  6.6 1.0 copy-start.2
  9.8 6.5 %copy-start.5 = (s32[128]{0:T(128)S(1)}, s32[128]{0:T(128)}, u32[]{:S(2)}) copy-start(s32[128]{0:T(128)} %param.26) | copy-start | bytes 1540
  9.9 21.4 %copy-start.4 = (bf16[4,2,4096]{2,1,0:T(2,128)(2,1)S(1)}, bf16[4,2,4096]{2,1,0:T(2,128)(2,1)}, u32[]{:S(2)}) copy-start(bf16[4,2,4096]{2,1,0:T(2,128)(2,1)} %param.24) | copy-start | bytes 196612
  16.9 25.3 %all-to-all-start.1 = ((s32[64,1,128]{2,1,0:T(1,128)}), s32[64,1,128]{2,1,0:T(1,128)S(1)}, u32[]{:S(2)}, u32[]{:S(2)}) async-start(s32[64,1,128]{2,1,0:T(1,128)} %broadcast_in_dim.8), calls=%async_computation.1 | async-start | bytes 65536 | tf_op jit(solution)/shard_map/all_to_all | solution.py:275
  42.3 0.6 copy-start.3
  42.9 24.5 %all-to-all-start = ((bf16[64,24,128]{2,1,0:T(8,128)(2,1)}), bf16[64,24,128]{2,1,0:T(8,128)(2,1)S(1)}, u32[]{:S(2)}, u32[]{:S(2)}) async-start(bf16[64,24,128]{2,1,0:T(8,128)(2,1)} %forward_z.1), calls=%async_computation | async-start | bytes 786432 | tf_op jit(solution)/shard_map/all_to_all | solution.py:276
  67.4 6.8 %copy-start.1 = (bf16[64,24,128]{2,1,0:T(8,128)(2,1)}, bf16[64,24,128]{2,1,0:T(8,128)(2,1)S(1)}, u32[]{:S(2)}) copy-start(bf16[64,24,128]{2,1,0:T(8,128)(2,1)S(1)} %all-to-all-done.recv) | copy-start | bytes 1179652
  67.4 31.7 %all-to-all-start.4 = ((f32[64,1,2,4]{3,2,1,0:T(2,128)}), f32[64,1,2,4]{3,2,1,0:T(2,128)S(1)}, u32[]{:S(2)}, u32[]{:S(2)}) async-start(f32[64,1,2,4]{3,2,1,0:T(2,128)} %bitcast.11), calls=%async_computation.4 | async-start | bytes 131072 | tf_op jit(solution)/shard_map/all_to_all | solution.py:308
  99.0 27.1 %all-to-all-start.2 = ((bf16[64,24,128]{2,1,0:T(8,128)(2,1)}), bf16[64,24,128]{2,1,0:T(8,128)(2,1)S(1)}, u32[]{:S(2)}, u32[]{:S(2)}) async-start(bf16[64,24,128]{2,1,0:T(8,128)(2,1)} %planes.1), calls=%async_computation.2 | async-start | bytes 786432 | tf_op jit(solution)/shard_map/all_to_all | solution.py:290
  126.1 0.7 copy-start
